TPU v7x, 32 devices: a whole 2x2x4 slice. The times are simulated.
32 devices in a mesh: gx: 4 (over x, core), gy: 2 (over y), gz: 4 (over z).
Axes of the slice: x: 2, y: 2, z: 4, core: 2. Of those that a mesh axis runs over, the one named last changes fastest.
Arguments:
- warped_image: float32 [256, 128, 512], P('gx', 'gy', 'gz'), may hold values from -6 to 6
- fixed_image: float32 [256, 128, 512], P('gx', 'gy', 'gz'), may hold values from -6 to 6
- fine_control: float32 [3, 32, 16, 64], P(None, 'gx', 'gy', 'gz'), may hold values from -6 to 6
- coarse_control: float32 [3, 8, 4, 16], replicated, may hold values from -6 to 6
Outputs:
- fine_gradient: float32 [3, 32, 16, 64], P(None, 'gx', 'gy', 'gz')
- coarse_gradient: float32 [3, 8, 4, 16], replicated
All inputs are finite; a program needn't handle non-finite values.
Results may differ from a plain program's by a relative error of at most 0.0003.
Values sent between devices are 32-bit elements; how exact they have to be, the bound alone decides.
A program may use at most 64 MiB of HBM per device.

v0:
```python
import jax
import jax.numpy as jnp
from jax import lax
from jax.sharding import PartitionSpec as P

SPF = 8
SPC = 32


bend_factor = 0.01
highest = lax.Precision.HIGHEST


def padded_2(block, sides, width):
    for axis, dim in sides:
        count = lax.axis_size(axis)
        forward = [(i, i + 1) for i in range(count - 1)]
        backward = [(target, source) for source, target in forward]
        low = lax.ppermute(
            lax.slice_in_dim(block, block.shape[dim] - width, None, axis=dim), axis, forward
        )
        high = lax.ppermute(lax.slice_in_dim(block, 0, width, axis=dim), axis, backward)
        block = jnp.concatenate([low, block, high], axis=dim)
    return block


def spline(values):
    magnitude = jnp.abs(values)
    inner = 2.0 / 3.0 - magnitude * magnitude + 0.5 * magnitude * magnitude * magnitude
    remain = 2.0 - magnitude
    outer = remain * remain * remain / 6.0
    return jnp.where(magnitude < 1.0, inner, jnp.where(magnitude < 2.0, outer, 0.0 * magnitude))


def basis_matrix(voxels, points, spacing, voxel_start, point_start):
    voxel = (jnp.arange(voxels, dtype=jnp.int32) + voxel_start).astype(jnp.float32) + 0.5
    centre = (jnp.arange(points, dtype=jnp.int32) + point_start).astype(
        jnp.float32
    ) * spacing + 0.5 * spacing
    return spline((voxel[:, None] - centre[None, :]) / spacing)


def slope(padded, axis):
    rank = padded.ndim
    count = padded.shape[axis] - 4

    def shifted(offset):
        piece = lax.slice_in_dim(padded, offset, offset + count, axis=axis)
        for other in range(rank - 3, rank):
            if other != axis:
                piece = lax.slice_in_dim(piece, 2, piece.shape[other] - 2, axis=other)
        return piece

    return (shifted(0) - 8.0 * shifted(1) + 8.0 * shifted(3) - shifted(4)) / 12.0


def stencil(padded):
    centre = padded[:, 1:-1, 1:-1, 1:-1]
    total = padded[:, 2:, 1:-1, 1:-1] + padded[:, :-2, 1:-1, 1:-1]
    total = total + padded[:, 1:-1, 2:, 1:-1] + padded[:, 1:-1, :-2, 1:-1]
    total = total + padded[:, 1:-1, 1:-1, 2:] + padded[:, 1:-1, 1:-1, :-2]
    return total - 6.0 * centre


def laplace(field):
    return stencil(jnp.pad(field, ((0, 0), (1, 1), (1, 1), (1, 1))))


def project(force, along_x, along_y, along_z):
    section = jnp.einsum("axyz,xp->apyz", force, along_x, precision=highest)
    section = jnp.einsum("apyz,yq->apqz", section, along_y, precision=highest)
    return jnp.einsum("apqz,zr->apqr", section, along_z, precision=highest)


def settle(extended, axis, points):
    own_part = lax.slice_in_dim(extended, 4, points + 4, axis=axis)
    from_left = lax.slice_in_dim(extended, 0, 2, axis=axis)
    from_right = lax.slice_in_dim(extended, points + 6, points + 8, axis=axis)
    leading = [(0, 0)] * extended.ndim
    trailing = [(0, 0)] * extended.ndim
    leading[axis] = (0, points - 2)
    trailing[axis] = (points - 2, 0)
    return own_part + jnp.pad(from_left, leading) + jnp.pad(from_right, trailing)


def inside(position, points, devices):
    global_index = position * points - 1 + jnp.arange(points + 2, dtype=jnp.int32)
    return ((global_index >= 0) & (global_index < points * devices)).astype(jnp.float32)


def per_device(warped_image, fixed_image, fine_control, coarse_control):
    size_x, size_y, size_z = warped_image.shape
    difference = warped_image - fixed_image
    padded = padded_2(warped_image + fixed_image, (("gx", 0), ("gy", 1), ("gz", 2)), 2)
    slopes = [0.5 * slope(padded, axis) for axis in range(3)]
    force = jnp.stack(slopes) * difference[None]
    points_x = size_x // SPF
    points_y = size_y // SPF
    points_z = size_z // SPF
    part = project(
        force,
        basis_matrix(size_x, points_x + 4, SPF, 0, -2),
        basis_matrix(size_y, points_y + 4, SPF, 0, -2),
        basis_matrix(size_z, points_z + 4, SPF, 0, -2),
    )
    part = settle(padded_2(part, (("gx", 1),), 2), 1, points_x)
    part = settle(padded_2(part, (("gy", 2),), 2), 2, points_y)
    part = settle(padded_2(part, (("gz", 3),), 2), 3, points_z)
    control = padded_2(fine_control, (("gx", 1), ("gy", 2), ("gz", 3)), 2)
    first = stencil(control)
    valid_x = inside(lax.axis_index("gx"), points_x, lax.axis_size("gx"))
    valid_y = inside(lax.axis_index("gy"), points_y, lax.axis_size("gy"))
    valid_z = inside(lax.axis_index("gz"), points_z, lax.axis_size("gz"))
    region = valid_x[:, None, None] * valid_y[None, :, None] * valid_z[None, None, :]
    first = first * region[None]
    fine_gradient = part * SPF ** (-1.5) + bend_factor * stencil(first)
    coarse_x = basis_matrix(size_x, coarse_control.shape[1], SPC, lax.axis_index("gx") * size_x, 0)
    coarse_y = basis_matrix(size_y, coarse_control.shape[2], SPC, lax.axis_index("gy") * size_y, 0)
    coarse_z = basis_matrix(size_z, coarse_control.shape[3], SPC, lax.axis_index("gz") * size_z, 0)
    coarse_part = project(force, coarse_x, coarse_y, coarse_z)
    coarse_sum = lax.psum(coarse_part, ("gx", "gy", "gz"))
    coarse_gradient = coarse_sum * SPC ** (-1.5) + bend_factor * laplace(laplace(coarse_control))
    return (fine_gradient, coarse_gradient)


def solution(mesh):
    in_specs = (P("gx", "gy", "gz"), P("gx", "gy", "gz"), P(None, "gx", "gy", "gz"), P())
    out_specs = (P(None, "gx", "gy", "gz"), P())
    return jax.shard_map(
        per_device, mesh=mesh, in_specs=in_specs, out_specs=out_specs, check_vma=False
    )
```

profile of v0, /device:TPU:0, one launch (start us, length us, event | category | flops | bytes accessed | tf_op | source)
XLA Modules:
  0.0 158.9 jit_solution(8543917966219928136)
XLA Ops:
  0.7 4.4 %fusion.237 = (f32[64,64,128]{2,1,0:T(8,128)}, f32[64,64,128]{2,1,0:T(8,128)S(1)}) fusion(f32[64,64,128]{2,1,0:T(8,128)} %param.4, f32[64,64,128]{2,1,0:T(8,128)} %param.5), kind=kLoop, calls=%fused_computation.303 | loop fusion | flops 1048576 | bytes 8388608 | tf_op jit(solution)/shard_map/sub | solution.py:93
  5.1 2.4 %collective-permute-start = (f32[2,64,128]{2,1,0:T(8,128)S(1)}, f32[2,64,128]{2,1,0:T(8,128)S(1)}, u32[]{:S(2)}, u32[]{:S(2)}) collective-permute-start(f32[2,64,128]{2,1,0:T(8,128)S(1)} %get-tuple-element.16), channel_id=1, source_target_pairs={{0,8},{8,16},{16,24},{1,9},{9,17},{17,25},{2,10},{10,18},{18,26},{... | collective-permute-start | bytes 196616 | tf_op jit(solution)/shard_map/ppermute | solution.py:19
  7.5 1.3 collective-permute-start.1
  8.8 5.1 %collective-permute-start.12 = (f32[3,2,8,16]{3,2,1,0:T(8,128)S(1)}, f32[3,2,8,16]{3,2,1,0:T(8,128)S(1)}, u32[]{:S(2)}, u32[]{:S(2)}) collective-permute-start(f32[3,2,8,16]{3,2,1,0:T(8,128)S(1)} %get-tuple-element.29), channel_id=1, source_target_pairs={{0,8},{8,16},{16,24},{1,9},{9,17},{17,25},{2,10},{10,18},{18,26},{... | collective-permute-start | bytes 9224 | tf_op jit(solution)/shard_map/ppermute | solution.py:19
  14.0 1.3 collective-permute-start.13
  15.7 2.6 %collective-permute-done.13 = f32[3,2,8,16]{3,2,1,0:T(8,128)S(1)} collective-permute-done((f32[3,2,8,16]{3,2,1,0:T(8,128)S(1)}, f32[3,2,8,16]{3,2,1,0:T(8,128)S(1)}, u32[]{:S(2)}, u32[]{:S(2)}) %collective-permute-start.13) | collective-permute-done | bytes 3104 | tf_op jit(solution)/shard_map/ppermute | solution.py:22
  18.3 3.4 %collective-permute-start.14 = (f32[3,12,2,16]{3,2,1,0:T(2,128)S(1)}, f32[3,12,2,16]{3,2,1,0:T(2,128)S(1)}, u32[]{:S(2)}, u32[]{:S(2)}) collective-permute-start(f32[3,12,2,16]{3,2,1,0:T(2,128)S(1)} %get-tuple-element.24), channel_id=1, source_target_pairs={{0,4},{1,5},{2,6},{3,7},{8,12},{9,13},{10,14},{11,15},{16,20},{17,... | collective-permute-start | bytes 13832 | tf_op jit(solution)/shard_map/ppermute | solution.py:19
  21.8 1.3 collective-permute-start.15
  23.1 0.3 collective-permute-done.14
  23.4 4.2 %collective-permute-done.15 = f32[3,12,2,16]{3,2,1,0:T(2,128)S(1)} collective-permute-done((f32[3,12,2,16]{3,2,1,0:T(2,128)S(1)}, f32[3,12,2,16]{3,2,1,0:T(2,128)S(1)}, u32[]{:S(2)}, u32[]{:S(2)}) %collective-permute-start.15) | collective-permute-done | bytes 4640 | tf_op jit(solution)/shard_map/ppermute | solution.py:22
  27.8 3.5 %collective-permute-start.16 = (f32[3,12,12,2]{3,2,1,0:T(8,128)S(1)}, f32[3,12,12,2]{3,2,1,0:T(8,128)S(1)}, u32[]{:S(2)}, u32[]{:S(2)}) collective-permute-start(f32[3,12,12,2]{3,2,1,0:T(8,128)S(1)} %get-tuple-element.20), channel_id=1, source_target_pairs={{0,1},{1,2},{2,3},{4,5},{5,6},{6,7},{8,9},{9,10},{10,11},{12,13},{... | collective-permute-start | bytes 10376 | tf_op jit(solution)/shard_map/ppermute | solution.py:19
  31.3 1.3 collective-permute-start.17
  32.7 5.9 %collective-permute-done.16 = f32[3,12,12,2]{3,2,1,0:T(8,128)S(1)} collective-permute-done((f32[3,12,12,2]{3,2,1,0:T(8,128)S(1)}, f32[3,12,12,2]{3,2,1,0:T(8,128)S(1)}, u32[]{:S(2)}, u32[]{:S(2)}) %collective-permute-start.16) | collective-permute-done | bytes 3488 | tf_op jit(solution)/shard_map/ppermute | solution.py:19
  38.5 4.4 %collective-permute-done.17 = f32[3,12,12,2]{3,2,1,0:T(8,128)S(1)} collective-permute-done((f32[3,12,12,2]{3,2,1,0:T(8,128)S(1)}, f32[3,12,12,2]{3,2,1,0:T(8,128)S(1)}, u32[]{:S(2)}, u32[]{:S(2)}) %collective-permute-start.17) | collective-permute-done | bytes 3488 | tf_op jit(solution)/shard_map/ppermute | solution.py:22
  43.0 0.3 pad_maximum_fusion.15
  43.3 0.6 fusion.36
  44.0 1.6 collective-permute-start.2
  45.5 1.3 collective-permute-start.3
  46.8 2.2 %fusion.9 = f32[1,64,64,128]{3,2,1,0:T(8,128)} fusion(f32[64,64,128]{2,1,0:T(8,128)S(1)} %get-tuple-element.9, f32[2,64,128]{2,1,0:T(8,128)S(1)} %collective-permute-done.1, f32[2,64,128]{2,1,0:T(8,128)S(1)} %collective-permute-done), kind=kLoop, calls=%fused_computation.17 | loop fusion | flops 5242880 | bytes 4325376 | tf_op jit(solution)/shard_map/stack | solution.py:96
  49.0 2.7 %collective-permute-done.3 = f32[68,2,128]{2,1,0:T(2,128)S(1)} collective-permute-done((f32[68,2,128]{2,1,0:T(2,128)S(1)}, f32[68,2,128]{2,1,0:T(2,128)S(1)}, u32[]{:S(2)}, u32[]{:S(2)}) %collective-permute-start.3) | collective-permute-done | bytes 69664 | tf_op jit(solution)/shard_map/ppermute | solution.py:22
  51.7 0.4 pad_maximum_fusion.1
  52.1 3.0 %fusion.238 = (f32[68,68,2]{2,1,0:T(8,128)}, f32[68,68,2]{2,1,0:T(8,128)}) fusion(f32[68,68,128]{2,1,0:T(8,128)S(1)} %pad_maximum_fusion.1), kind=kLoop, calls=%fused_computation.304 | loop fusion | bytes 147968 | tf_op jit(solution)/shard_map/slice | solution.py:20
  55.1 2.6 %copy.19 = f32[68,68,2]{1,0,2:T(8,128)S(1)} copy(f32[68,68,2]{2,1,0:T(8,128)} %get-tuple-element.11) | data formatting | bytes 73984 | tf_op jit(solution)/shard_map/slice | solution.py:22
  57.7 1.3 collective-permute-start.5
  59.0 2.6 %copy.17 = f32[68,68,2]{1,2,0:T(2,128)S(1)} copy(f32[68,68,2]{2,1,0:T(8,128)} %get-tuple-element.10) | data formatting | bytes 73984 | tf_op jit(solution)/shard_map/slice | solution.py:20
  61.6 4.6 %collective-permute-start.4 = (f32[68,68,2]{1,2,0:T(2,128)S(1)}, f32[68,68,2]{1,2,0:T(2,128)S(1)}, u32[]{:S(2)}, u32[]{:S(2)}) collective-permute-start(f32[68,68,2]{1,2,0:T(2,128)S(1)} %copy.17), channel_id=1, source_target_pairs={{0,1},{1,2},{2,3},{4,5},{5,6},{6,7},{8,9},{9,10},{10,11},{12,13},{... | collective-permute-start | bytes 110984 | tf_op jit(solution)/shard_map/ppermute | solution.py:19
  66.2 0.4 maximum_maximum_fusion
  66.6 2.1 %fusion.19 = f32[1,64,64,128]{3,2,1,0:T(8,128)} fusion(f32[68,66,128]{2,1,0:T(8,128)S(1)} %get-tuple-element.13, f32[68,66,128]{2,1,0:T(8,128)S(1)} %get-tuple-element.12), kind=kLoop, calls=%fused_computation.39 | loop fusion | flops 3145728 | bytes 10485760 | tf_op jit(solution)/shard_map/stack | solution.py:96
  68.8 2.4 %copy.20 = f32[68,68,2]{2,1,0:T(8,128)} copy(f32[68,68,2]{1,0,2:T(8,128)S(1)} %collective-permute-done.5) | data formatting | bytes 73984 | tf_op jit(solution)/shard_map/ppermute | solution.py:22
  71.1 2.4 %copy.18 = f32[68,68,2]{2,1,0:T(8,128)} copy(f32[68,68,2]{1,2,0:T(2,128)S(1)} %collective-permute-done.4) | data formatting | bytes 73984 | tf_op jit(solution)/shard_map/ppermute | solution.py:19
  73.5 10.4 %fusion.14 = f32[1,64,64,128]{3,2,1,0:T(8,128)S(1)} fusion(f32[68,68,2]{2,1,0:T(8,128)} %copy.20, f32[68,2,128]{2,1,0:T(2,128)S(1)} %collective-permute-done.3, f32[68,2,128]{2,1,0:T(2,128)S(1)} %collective-permute-done.2, f32[2,64,128]{2,1,0:T(8,128)S(1)} %collective-permute-done.1, f32[64,64,128]{2,1,0:T(8,128)S(1)} %get-tuple-element.9, ...), kind=kLoop, calls=%fused_computation.23 | loop fusion | flops 13631488 | bytes 4538624 | tf_op jit(solution)/shard_map/stack | solution.py:96
  83.9 1.1 maximum_multiply_fusion
  85.0 6.5 %fusion.23 = f32[3,12,64,128]{3,1,2,0:T(8,128)S(1)} fusion(f32[3,64,64,128]{3,2,1,0:T(8,128)S(1)} %maximum_multiply_fusion, f32[12]{0:T(128)S(1)} %multiply_add_fusion.4, f32[64]{0:T(128)S(1)} %convert_add_fusion.4), kind=kOutput, calls=%fused_computation.47 | convolution fusion | flops 226506240 | bytes 7471408 | tf_op jit(solution)/shard_map/axyz,xp->apyz/dot_general | solution.py:70
  91.4 1.0 fusion.31
  92.4 0.5 fusion.65
  92.9 1.3 collective-permute-start.6
  94.2 1.5 collective-permute-start.7
  95.7 6.5 %fusion.26 = f32[3,8,64,128]{3,1,2,0:T(8,128)S(1)} fusion(f32[3,64,64,128]{3,2,1,0:T(8,128)S(1)} %maximum_multiply_fusion, f32[8]{0:T(128)S(1)} %multiply_add_fusion.1, f32[64]{0:T(128)S(1)} %convert_add_fusion.1), kind=kOutput, calls=%fused_computation.48 | convolution fusion | flops 151004160 | bytes 7078176 | tf_op jit(solution)/shard_map/axyz,xp->apyz/dot_general | solution.py:70
  102.2 0.6 convolution_bitcast_fusion
  102.9 1.8 %collective-permute-start.8 = (f32[3,8,2,20]{3,2,1,0:T(2,128)S(1)}, f32[3,8,2,20]{3,2,1,0:T(2,128)S(1)}, u32[]{:S(2)}, u32[]{:S(2)}) collective-permute-start(f32[3,8,2,20]{3,2,1,0:T(2,128)S(1)} %get-tuple-element.22), channel_id=1, source_target_pairs={{0,4},{1,5},{2,6},{3,7},{8,12},{9,13},{10,14},{11,15},{16,20},{17,... | collective-permute-start | bytes 11528 | tf_op jit(solution)/shard_map/ppermute | solution.py:19
  104.7 1.3 collective-permute-start.9
  106.0 0.2 fusion.60
  106.2 42.9 %psum.7 = f32[3,8,4,16]{3,1,2,0:T(8,128)S(1)} all-reduce(f32[3,8,4,16]{3,1,2,0:T(8,128)S(1)} %fusion.60), channel_id=1, replica_groups=mesh['gx'=4,'gy'=2,'gz'=4] {'gx','gy','gz'}, use_global_device_ids=true, to_apply=%region_0.1 | all-reduce | flops 1536 | bytes 12288 | tf_op jit(solution)/shard_map/psum | solution.py:121
  149.3 2.2 %collective-permute-start.10 = (f32[3,8,8,2]{3,2,1,0:T(8,128)S(1)}, f32[3,8,8,2]{3,2,1,0:T(8,128)S(1)}, u32[]{:S(2)}, u32[]{:S(2)}) collective-permute-start(f32[3,8,8,2]{3,2,1,0:T(8,128)S(1)} %get-tuple-element.26), channel_id=1, source_target_pairs={{0,1},{1,2},{2,3},{4,5},{5,6},{6,7},{8,9},{9,10},{10,11},{12,13},{... | collective-permute-start | bytes 4616 | tf_op jit(solution)/shard_map/ppermute | solution.py:19
  151.5 1.3 collective-permute-start.11
  152.9 0.6 copy.28
  153.7 4.3 %collective-permute-done.11 = f32[3,8,8,2]{3,2,1,0:T(8,128)S(1)} collective-permute-done((f32[3,8,8,2]{3,2,1,0:T(8,128)S(1)}, f32[3,8,8,2]{3,2,1,0:T(8,128)S(1)}, u32[]{:S(2)}, u32[]{:S(2)}) %collective-permute-start.11) | collective-permute-done | bytes 1568 | tf_op jit(solution)/shard_map/ppermute | solution.py:22
  158.0 0.9 fusion.42
  (52 shorter events, 1.1 us)
Async XLA Ops:
  0.6 8.2 %copy-start.3 = (f32[3,8,8,16]{3,2,1,0:T(8,128)S(1)}, f32[3,8,8,16]{3,2,1,0:T(8,128)}, u32[]{:S(2)}) copy-start(f32[3,8,8,16]{3,2,1,0:T(8,128)} %param.6) | copy-start | bytes 36868
  0.6 14.7 %copy-start.4 = (f32[3,8,4,16]{3,2,1,0:T(4,128)S(1)}, f32[3,8,4,16]{3,2,1,0:T(4,128)}, u32[]{:S(2)}) copy-start(f32[3,8,4,16]{3,2,1,0:T(4,128)} %param.7) | copy-start | bytes 18436
  5.1 38.8 %collective-permute-start = (f32[2,64,128]{2,1,0:T(8,128)S(1)}, f32[2,64,128]{2,1,0:T(8,128)S(1)}, u32[]{:S(2)}, u32[]{:S(2)}) collective-permute-start(f32[2,64,128]{2,1,0:T(8,128)S(1)} %get-tuple-element.16), channel_id=1, source_target_pairs={{0,8},{8,16},{16,24},{1,9},{9,17},{17,25},{2,10},{10,18},{18,26},{... | collective-permute-start | bytes 196616 | tf_op jit(solution)/shard_map/ppermute | solution.py:19
  7.5 36.4 %collective-permute-start.1 = (f32[2,64,128]{2,1,0:T(8,128)S(1)}, f32[2,64,128]{2,1,0:T(8,128)S(1)}, u32[]{:S(2)}, u32[]{:S(2)}) collective-permute-start(f32[2,64,128]{2,1,0:T(8,128)S(1)} %get-tuple-element.17), channel_id=1, source_target_pairs={{8,0},{16,8},{24,16},{9,1},{17,9},{25,17},{10,2},{18,10},{26,18},{... | collective-permute-start | bytes 196616 | tf_op jit(solution)/shard_map/ppermute | solution.py:22
  8.8 6.9 %collective-permute-start.12 = (f32[3,2,8,16]{3,2,1,0:T(8,128)S(1)}, f32[3,2,8,16]{3,2,1,0:T(8,128)S(1)}, u32[]{:S(2)}, u32[]{:S(2)}) collective-permute-start(f32[3,2,8,16]{3,2,1,0:T(8,128)S(1)} %get-tuple-element.29), channel_id=1, source_target_pairs={{0,8},{8,16},{16,24},{1,9},{9,17},{17,25},{2,10},{10,18},{18,26},{... | collective-permute-start | bytes 9224 | tf_op jit(solution)/shard_map/ppermute | solution.py:19
  14.0 4.3 %collective-permute-start.13 = (f32[3,2,8,16]{3,2,1,0:T(8,128)S(1)}, f32[3,2,8,16]{3,2,1,0:T(8,128)S(1)}, u32[]{:S(2)}, u32[]{:S(2)}) collective-permute-start(f32[3,2,8,16]{3,2,1,0:T(8,128)S(1)} %get-tuple-element.28), channel_id=1, source_target_pairs={{8,0},{16,8},{24,16},{9,1},{17,9},{25,17},{10,2},{18,10},{26,18},{... | collective-permute-start | bytes 9224 | tf_op jit(solution)/shard_map/ppermute | solution.py:22
  18.3 5.0 %collective-permute-start.14 = (f32[3,12,2,16]{3,2,1,0:T(2,128)S(1)}, f32[3,12,2,16]{3,2,1,0:T(2,128)S(1)}, u32[]{:S(2)}, u32[]{:S(2)}) collective-permute-start(f32[3,12,2,16]{3,2,1,0:T(2,128)S(1)} %get-tuple-element.24), channel_id=1, source_target_pairs={{0,4},{1,5},{2,6},{3,7},{8,12},{9,13},{10,14},{11,15},{16,20},{17,... | collective-permute-start | bytes 13832 | tf_op jit(solution)/shard_map/ppermute | solution.py:19
  21.8 5.9 %collective-permute-start.15 = (f32[3,12,2,16]{3,2,1,0:T(2,128)S(1)}, f32[3,12,2,16]{3,2,1,0:T(2,128)S(1)}, u32[]{:S(2)}, u32[]{:S(2)}) collective-permute-start(f32[3,12,2,16]{3,2,1,0:T(2,128)S(1)} %get-tuple-element.25), channel_id=1, source_target_pairs={{4,0},{5,1},{6,2},{7,3},{12,8},{13,9},{14,10},{15,11},{20,16},{21,... | collective-permute-start | bytes 13832 | tf_op jit(solution)/shard_map/ppermute | solution.py:22
  27.8 10.7 %collective-permute-start.16 = (f32[3,12,12,2]{3,2,1,0:T(8,128)S(1)}, f32[3,12,12,2]{3,2,1,0:T(8,128)S(1)}, u32[]{:S(2)}, u32[]{:S(2)}) collective-permute-start(f32[3,12,12,2]{3,2,1,0:T(8,128)S(1)} %get-tuple-element.20), channel_id=1, source_target_pairs={{0,1},{1,2},{2,3},{4,5},{5,6},{6,7},{8,9},{9,10},{10,11},{12,13},{... | collective-permute-start | bytes 10376 | tf_op jit(solution)/shard_map/ppermute | solution.py:19
  31.3 11.7 %collective-permute-start.17 = (f32[3,12,12,2]{3,2,1,0:T(8,128)S(1)}, f32[3,12,12,2]{3,2,1,0:T(8,128)S(1)}, u32[]{:S(2)}, u32[]{:S(2)}) collective-permute-start(f32[3,12,12,2]{3,2,1,0:T(8,128)S(1)} %get-tuple-element.21), channel_id=1, source_target_pairs={{1,0},{2,1},{3,2},{5,4},{6,5},{7,6},{9,8},{10,9},{11,10},{13,12},{... | collective-permute-start | bytes 10376 | tf_op jit(solution)/shard_map/ppermute | solution.py:22
  44.0 5.1 %collective-permute-start.2 = (f32[68,2,128]{2,1,0:T(2,128)S(1)}, f32[68,2,128]{2,1,0:T(2,128)S(1)}, u32[]{:S(2)}, u32[]{:S(2)}) collective-permute-start(f32[68,2,128]{2,1,0:T(2,128)S(1)} %get-tuple-element.14), channel_id=1, source_target_pairs={{0,4},{1,5},{2,6},{3,7},{8,12},{9,13},{10,14},{11,15},{16,20},{17,... | collective-permute-start | bytes 208904 | tf_op jit(solution)/shard_map/ppermute | solution.py:19
  45.5 6.2 %collective-permute-start.3 = (f32[68,2,128]{2,1,0:T(2,128)S(1)}, f32[68,2,128]{2,1,0:T(2,128)S(1)}, u32[]{:S(2)}, u32[]{:S(2)}) collective-permute-start(f32[68,2,128]{2,1,0:T(2,128)S(1)} %get-tuple-element.15), channel_id=1, source_target_pairs={{4,0},{5,1},{6,2},{7,3},{12,8},{13,9},{14,10},{15,11},{20,16},{21,... | collective-permute-start | bytes 208904 | tf_op jit(solution)/shard_map/ppermute | solution.py:22
  57.7 11.0 %collective-permute-start.5 = (f32[68,68,2]{1,0,2:T(8,128)S(1)}, f32[68,68,2]{1,0,2:T(8,128)S(1)}, u32[]{:S(2)}, u32[]{:S(2)}) collective-permute-start(f32[68,68,2]{1,0,2:T(8,128)S(1)} %copy.19), channel_id=1, source_target_pairs={{1,0},{2,1},{3,2},{5,4},{6,5},{7,6},{9,8},{10,9},{11,10},{13,12},{... | collective-permute-start | bytes 110984 | tf_op jit(solution)/shard_map/ppermute | solution.py:22
  61.6 9.5 %collective-permute-start.4 = (f32[68,68,2]{1,2,0:T(2,128)S(1)}, f32[68,68,2]{1,2,0:T(2,128)S(1)}, u32[]{:S(2)}, u32[]{:S(2)}) collective-permute-start(f32[68,68,2]{1,2,0:T(2,128)S(1)} %copy.17), channel_id=1, source_target_pairs={{0,1},{1,2},{2,3},{4,5},{5,6},{6,7},{8,9},{9,10},{10,11},{12,13},{... | collective-permute-start | bytes 110984 | tf_op jit(solution)/shard_map/ppermute | solution.py:19
  73.5 10.4 %copy-start = (f32[1,64,64,128]{3,2,1,0:T(8,128)S(1)}, f32[1,64,64,128]{3,2,1,0:T(8,128)}, u32[]{:S(2)}) copy-start(f32[1,64,64,128]{3,2,1,0:T(8,128)} %fusion.19) | copy-start | bytes 6291460
  73.5 10.4 %copy-start.1 = (f32[1,64,64,128]{3,2,1,0:T(8,128)S(1)}, f32[1,64,64,128]{3,2,1,0:T(8,128)}, u32[]{:S(2)}) copy-start(f32[1,64,64,128]{3,2,1,0:T(8,128)} %fusion.9) | copy-start | bytes 6291460
  73.5 10.4 %copy-start.2 = (f32[64,64,128]{2,1,0:T(8,128)S(1)}, f32[64,64,128]{2,1,0:T(8,128)}, u32[]{:S(2)}) copy-start(f32[64,64,128]{2,1,0:T(8,128)} %get-tuple-element.8) | copy-start | bytes 6291460
  92.9 9.9 %collective-permute-start.6 = (f32[3,2,12,20]{3,2,1,0:T(8,128)S(1)}, f32[3,2,12,20]{3,2,1,0:T(8,128)S(1)}, u32[]{:S(2)}, u32[]{:S(2)}) collective-permute-start(f32[3,2,12,20]{3,2,1,0:T(8,128)S(1)} %get-tuple-element.18), channel_id=1, source_target_pairs={{0,8},{8,16},{16,24},{1,9},{9,17},{17,25},{2,10},{10,18},{18,26},{... | collective-permute-start | bytes 17288 | tf_op jit(solution)/shard_map/ppermute | solution.py:19
  94.2 8.6 %collective-permute-start.7 = (f32[3,2,12,20]{3,2,1,0:T(8,128)S(1)}, f32[3,2,12,20]{3,2,1,0:T(8,128)S(1)}, u32[]{:S(2)}, u32[]{:S(2)}) collective-permute-start(f32[3,2,12,20]{3,2,1,0:T(8,128)S(1)} %get-tuple-element.19), channel_id=1, source_target_pairs={{8,0},{16,8},{24,16},{9,1},{17,9},{25,17},{10,2},{18,10},{26,18},{... | collective-permute-start | bytes 17288 | tf_op jit(solution)/shard_map/ppermute | solution.py:22
  102.9 46.3 %collective-permute-start.8 = (f32[3,8,2,20]{3,2,1,0:T(2,128)S(1)}, f32[3,8,2,20]{3,2,1,0:T(2,128)S(1)}, u32[]{:S(2)}, u32[]{:S(2)}) collective-permute-start(f32[3,8,2,20]{3,2,1,0:T(2,128)S(1)} %get-tuple-element.22), channel_id=1, source_target_pairs={{0,4},{1,5},{2,6},{3,7},{8,12},{9,13},{10,14},{11,15},{16,20},{17,... | collective-permute-start | bytes 11528 | tf_op jit(solution)/shard_map/ppermute | solution.py:19
  104.7 44.5 %collective-permute-start.9 = (f32[3,8,2,20]{3,2,1,0:T(2,128)S(1)}, f32[3,8,2,20]{3,2,1,0:T(2,128)S(1)}, u32[]{:S(2)}, u32[]{:S(2)}) collective-permute-start(f32[3,8,2,20]{3,2,1,0:T(2,128)S(1)} %get-tuple-element.23), channel_id=1, source_target_pairs={{4,0},{5,1},{6,2},{7,3},{12,8},{13,9},{14,10},{15,11},{20,16},{21,... | collective-permute-start | bytes 11528 | tf_op jit(solution)/shard_map/ppermute | solution.py:22
  149.3 4.4 %collective-permute-start.10 = (f32[3,8,8,2]{3,2,1,0:T(8,128)S(1)}, f32[3,8,8,2]{3,2,1,0:T(8,128)S(1)}, u32[]{:S(2)}, u32[]{:S(2)}) collective-permute-start(f32[3,8,8,2]{3,2,1,0:T(8,128)S(1)} %get-tuple-element.26), channel_id=1, source_target_pairs={{0,1},{1,2},{2,3},{4,5},{5,6},{6,7},{8,9},{9,10},{10,11},{12,13},{... | collective-permute-start | bytes 4616 | tf_op jit(solution)/shard_map/ppermute | solution.py:19
  151.5 6.5 %collective-permute-start.11 = (f32[3,8,8,2]{3,2,1,0:T(8,128)S(1)}, f32[3,8,8,2]{3,2,1,0:T(8,128)S(1)}, u32[]{:S(2)}, u32[]{:S(2)}) collective-permute-start(f32[3,8,8,2]{3,2,1,0:T(8,128)S(1)} %get-tuple-element.27), channel_id=1, source_target_pairs={{1,0},{2,1},{3,2},{5,4},{6,5},{7,6},{9,8},{10,9},{11,10},{13,12},{... | collective-permute-start | bytes 4616 | tf_op jit(solution)/shard_map/ppermute | solution.py:22
where the time goes:
time: 160 us; the launch traced here: 159 us
  blocking collectives  42.9 us (27%)
  starting transfers between devices  37.7 us (24%)
  waiting for transfers between devices  24.6 us (15%)
  other arithmetic  23.4 us (15%)
  matrix products  15.2 us (10%)
  local copies, waits for them, and re-layouts  13.9 us (9%)
    psum x1, blocking collectives, per_device(): coarse_sum = lax.psum(coarse_part, ('gx', 'gy', 'gz'))  42.9 us
    ppermute x9, starting transfers between devices, padded_2(): lax.ppermute(lax.slice_in_dim(block, block.shape[dim] - width, None, axis...  25.9 us
    ppermute x9, waiting for transfers between devices, padded_2(): lax.ppermute(lax.slice_in_dim(block, 0, width, axis=dim), axis, backward)  18.3 us
    another operation x3, other arithmetic, per_device(): force = jnp.stack(slopes) * difference[None]  14.7 us
    dot_general x2, matrix products, project(): section = jnp.einsum('axyz,xp->apyz', force, along_x, precision=highest)  13 us
    ppermute x9, starting transfers between devices, padded_2(): lax.ppermute(lax.slice_in_dim(block, 0, width, axis=dim), axis, backward)  11.9 us
    ppermute x9, waiting for transfers between devices, padded_2(): lax.ppermute(lax.slice_in_dim(block, block.shape[dim] - width, None, axis...  6.36 us
    slice x8, local copies, waits for them, and re-layouts, padded_2(): lax.slice_in_dim(block, block.shape[dim] - width, None, axis=dim)  5.86 us
  transfers between devices with their start and end apart: 18, of which 8 were waited for; matrix products, arithmetic and copies ran while one was open for 12% of the time, Pallas kernels for 0%

commit v1 on v0

v1 whole, which is shorter than its diff:
```python
import functools

import jax
import jax.numpy as jnp
from jax import lax
from jax.experimental import pallas as pl
from jax.experimental.pallas import tpu as pltpu
from jax.sharding import PartitionSpec as P

SPF = 8
SPC = 32
BEND = 0.01
HI = lax.Precision.HIGHEST
MESH = pl.DeviceIdType.MESH
f32 = jnp.float32
bf16 = jnp.bfloat16


def nn(a, b):
    return lax.dot_general(
        a, b, (((1,), (0,)), ((), ())), precision=HI, preferred_element_type=f32
    )


def nt(a, b):
    return lax.dot_general(
        a, b, (((1,), (1,)), ((), ())), precision=HI, preferred_element_type=f32
    )


def spline(t):
    m = jnp.abs(t)
    inner = 2.0 / 3.0 - m * m + 0.5 * m * m * m
    r = 2.0 - m
    outer = r * r * r * (1.0 / 6.0)
    return jnp.where(m < 1.0, inner, jnp.where(m < 2.0, outer, 0.0))


def weight(voxel, point, spacing):
    scaled = (2 * voxel + 1 - spacing * (2 * point + 1)).astype(f32)
    return spline(scaled * (0.5 / spacing))


def iota(shape, axis):
    return lax.broadcasted_iota(jnp.int32, shape, axis)


def diff1(out, inp):
    d = jnp.abs(out - inp)
    return jnp.where(d == 0, -2.0, jnp.where(d == 1, 1.0, 0.0)).astype(f32)


def diff2(out, inp, count):
    d = jnp.abs(out - inp)
    edge = (inp == 0) | (inp == count - 1)
    centre = jnp.where(edge, 5.0, 6.0)
    return jnp.where(
        d == 0, centre, jnp.where(d == 1, -4.0, jnp.where(d == 2, 1.0, 0.0))
    ).astype(f32)


def same(out, inp):
    return jnp.where(out == inp, 1.0, 0.0).astype(f32)


def bend_planes(px, py, qx, qy, cx, cy):
    jx, jy = same(px, qx), same(py, qy)
    tx, ty = diff1(px, qx), diff1(py, qy)
    m0 = diff2(px, qx, cx) * jy + jx * diff2(py, qy, cy) + 2.0 * tx * ty
    m1 = 2.0 * (tx * jy + jx * ty)
    return m0 * BEND, m1 * BEND, jx * jy * BEND


def kernel(sizes, w_hbm, f_hbm, fc_ref, cc_ref, fo_ref, co_ref,
           w_v, f_v, s_v, ysend, yrecv, zsend, zrecv, zcorr, wf_v, wc_v, fh_v, fl_v,
           accf, accc, tz_v, bend_v, ccp, bendc, zmsg, zgot, a_v, agot, b_v, bgot,
           cslots, load_sem, hs_sem, hr_sem, ms_sem, mr_sem, cs_sem, cr_sem):
    nx, ny, nz = sizes
    axes = ("gx", "gy", "gz")
    counts = sizes
    me = [lax.axis_index(a) for a in axes]
    SX, SY, SZ = w_v.shape
    PX, PY, PZ = SX // SPF, SY // SPF, SZ // SPF
    EX, QE, QC = PX + 4, 16, accc.shape[1]
    KX, KY, KZ = cc_ref.shape[1:]
    cells = SX // SPF
    lanes = 3 * SZ

    loads = []
    for c in range(cells):
        part = pl.ds(c * SPF, SPF)
        loads.append((
            pltpu.make_async_copy(w_hbm.at[part], w_v.at[part], load_sem.at[0, c]),
            pltpu.make_async_copy(f_hbm.at[part], f_v.at[part], load_sem.at[1, c]),
        ))
    for one, two in loads:
        one.start()
        two.start()

    zero_plane = jnp.zeros((2, SY, SZ), f32)
    s_v[0:2, 8:8 + SY, :] = zero_plane
    s_v[SX + 2:SX + 4, 8:8 + SY, :] = zero_plane
    yrecv[...] = jnp.zeros(yrecv.shape, f32)
    zrecv[...] = jnp.zeros(zrecv.shape, f32)
    zgot[...] = jnp.zeros(zgot.shape, f32)
    agot[...] = jnp.zeros(agot.shape, f32)
    bgot[...] = jnp.zeros(bgot.shape, f32)

    barrier = pltpu.get_barrier_semaphore()
    total = 0
    for k, a in enumerate(axes):
        for d in range(1, counts[k]):
            pl.semaphore_signal(
                barrier, inc=1, device_id={a: lax.rem(me[k] + d, counts[k])}, device_id_type=MESH
            )
            total += 1

    def split_store(ref, index, value):
        high = value.astype(bf16)
        ref[index + (0,)] = high
        ref[index + (1,)] = (value - high.astype(f32)).astype(bf16)

    KC = SPF * SY
    rows, cols = iota((5 * QE, KC), 0), iota((5 * QE, KC), 1)
    split_store(wf_v, (), weight(cols // SY, rows // QE - 2, SPF)
                * weight(cols % SY, rows % QE - 2, SPF))
    rows, cols = iota((4 * QC, KC), 0), iota((4 * QC, KC), 1)
    along_y = weight(cols % SY + me[1] * SY, rows % QC, SPC)
    for ph in range(SPC // SPF):
        first = -2 if ph < SPC // SPF // 2 else -1
        split_store(wc_v, (ph,),
                    weight(cols // SY + ph * SPF, rows // QC + first, SPC) * along_y)

    lane = iota((SY, SZ), 1)

    def one_slab(x, carry):
        low, high = carry
        s = w_v[x] + f_v[x]
        s_v[x + 2, 8:8 + SY, :] = s
        ysend[0, x] = s[0:2]
        ysend[1, x] = s[SY - 2:SY]
        here = lane // 2 == x
        low = jnp.where(here, pltpu.roll(s, 2 * x, 1), low)
        high = jnp.where(here, pltpu.roll(s, lax.rem(2 * x + 2, SZ), 1), high)
        return low, high

    carry = (jnp.zeros((SY, SZ), f32), jnp.zeros((SY, SZ), f32))
    for c in range(cells):
        for copy in loads[c]:
            copy.wait()
        carry = lax.fori_loop(c * SPF, (c + 1) * SPF, one_slab, carry)
    zsend[0] = carry[0]
    zsend[1] = carry[1]

    pl.semaphore_wait(barrier, total)

    has = [(me[k] > 0, me[k] < counts[k] - 1) for k in range(3)]

    def halo(k, side):
        if k == 0:
            src = s_v.at[pl.ds(2 if side == 0 else SX, 2), pl.ds(8, SY), :]
            dst = s_v.at[pl.ds(SX + 2 if side == 0 else 0, 2), pl.ds(8, SY), :]
        elif k == 1:
            src, dst = ysend.at[side], yrecv.at[1 - side]
        else:
            src, dst = zsend.at[side], zrecv.at[1 - side]
        return neighbour_copy(k, side, src, dst, hs_sem.at[k, side], hr_sem.at[k, 1 - side])

    def neighbour_copy(k, side, src, dst, send, recv):
        other = me[k] - 1 if side == 0 else me[k] + 1
        return pltpu.make_async_remote_copy(
            src_ref=src, dst_ref=dst, send_sem=send, recv_sem=recv,
            device_id={axes[k]: other}, device_id_type=MESH,
        )

    for k in (2, 1, 0):
        for side in range(2):
            @pl.when(has[k][side])
            def _(k=k, side=side):
                halo(k, side).start()

    accf[...] = jnp.zeros(accf.shape, f32)
    accc[...] = jnp.zeros(accc.shape, f32)
    shape = (EX * QE, PX * PY)
    rows, cols = iota(shape, 0), iota(shape, 1)
    ox, oy = me[0] * PX, me[1] * PY
    planes = bend_planes(rows // QE - 2 + ox, rows % QE - 2 + oy,
                         cols // PY + ox, cols % PY + oy, PX * nx, PY * ny)
    RZ = tz_v.shape[1]

    def ext_point(row):
        return jnp.where(row < PZ, row, jnp.where(row < PZ + 2, row - PZ - 2, row - 2))

    oz = me[2] * PZ
    zr, zc = ext_point(iota((RZ, PZ), 0)) + oz, iota((RZ, PZ), 1) + oz
    along = (same(zr, zc), diff1(zr, zc), diff2(zr, zc, PZ * nz))
    for a in range(3):
        block = fc_ref[a].reshape(PX * PY, PZ)
        bend_v[a] = (nt(along[0], nn(planes[0], block)) + nt(along[1], nn(planes[1], block))
                     + nt(along[2], nn(planes[2], block)))
    shape = (KX * QC, KX * QC)
    rows, cols = iota(shape, 0), iota(shape, 1)
    planes = bend_planes(rows // QC, rows % QC, cols // QC, cols % QC, KX, KY)
    zr, zc = iota((KZ, KZ), 0), iota((KZ, KZ), 1)
    ccp[...] = jnp.zeros(ccp.shape, f32)
    for a in range(3):
        for p in range(KX):
            ccp[a, p * QC:p * QC + KY, :] = cc_ref[a, p]
        block = ccp[a]
        bendc[a] = (nn(planes[0], block) + nn(planes[1], nn(block, diff1(zr, zc)))
                    + BEND * nn(block, diff2(zr, zc, KZ)))

    for k in (2, 1, 0):
        for side in range(2):
            @pl.when(has[k][side])
            def _(k=k, side=side):
                copy = halo(k, side)
                copy.wait_send()

            @pl.when(has[k][1 - side])
            def _(k=k, side=side):
                halo(k, side).wait_recv()

    even = lane % 2 == 0
    dl = zrecv[0] - zsend[1]
    dh = zrecv[1] - zsend[0]
    zcorr[0] = jnp.where(even, dl - 8.0 * pltpu.roll(dl, SZ - 1, 1), dl)
    zcorr[1] = jnp.where(even, -dh, 8.0 * pltpu.roll(dh, 1, 1) - dh)

    def cell(i, _):
        k = i // (SPC // SPF)
        ph = i % (SPC // SPF)
        for xx in range(SPF):
            x = i * SPF + xx
            s_v[x + 2, 6:8, :] = yrecv[0, x]
            s_v[x + 2, 8 + SY:10 + SY, :] = yrecv[1, x]
            d = w_v[x] - f_v[x]
            s = s_v[x + 2, 8:8 + SY, :]
            gx = (s_v[x, 8:8 + SY, :] - s_v[x + 4, 8:8 + SY, :]
                  + 8.0 * (s_v[x + 3, 8:8 + SY, :] - s_v[x + 1, 8:8 + SY, :]))
            gy = (s_v[x + 2, 6:6 + SY, :] - s_v[x + 2, 10:10 + SY, :]
                  + 8.0 * (s_v[x + 2, 9:9 + SY, :] - s_v[x + 2, 7:7 + SY, :]))
            gz = (pltpu.roll(s, 2, 1) - pltpu.roll(s, SZ - 2, 1)
                  + 8.0 * (pltpu.roll(s, SZ - 1, 1) - pltpu.roll(s, 1, 1)))
            corr = jnp.where(lane < 2, pltpu.roll(zcorr[0], lax.rem(SZ - 2 * x, SZ), 1), 0.0)
            corr = jnp.where(lane >= SZ - 2,
                             pltpu.roll(zcorr[1], lax.rem(2 * SZ - 2 - 2 * x, SZ), 1), corr)
            gz = gz + corr
            for a, g in enumerate((gx, gy, gz)):
                force = g * d
                high = force.astype(bf16)
                fh_v[xx * SY:(xx + 1) * SY, a * SZ:(a + 1) * SZ] = high
                fl_v[xx * SY:(xx + 1) * SY, a * SZ:(a + 1) * SZ] = (
                    force - high.astype(f32)).astype(bf16)
        wh = jnp.concatenate([wf_v[0], wc_v[ph, 0]], axis=0)
        wl = jnp.concatenate([wf_v[1], wc_v[ph, 1]], axis=0)
        out = (jnp.dot(wh, fh_v[...], preferred_element_type=f32)
               + jnp.dot(wl, fh_v[...], preferred_element_type=f32)
               + jnp.dot(wh, fl_v[...], preferred_element_type=f32))
        accf[pl.ds(i, 5)] += out[:5 * QE].reshape(5, QE, lanes)
        at = me[0] * (SX // SPC) + k + jnp.where(ph >= SPC // SPF // 2, 1, 0)
        accc[pl.ds(at, 4)] += out[5 * QE:].reshape(4, QC, lanes)
        return 0

    lax.fori_loop(0, cells, cell, 0)

    rows, cols = iota((RZ, SZ), 0), iota((RZ, SZ), 1)
    bz = weight(cols, ext_point(rows), SPF) * (SPF ** -1.5 / 24.0)
    rows, cols = iota((KZ, SZ), 0), iota((KZ, SZ), 1)
    bzc = weight(cols + me[2] * SZ, rows, SPC) * (SPC ** -1.5 / 24.0)
    zmsg[...] = jnp.zeros(zmsg.shape, f32)
    for a in range(3):
        block = accf[:, :, a * SZ:(a + 1) * SZ].reshape(EX * QE, SZ)
        tz_v[a] = nt(bz, block) + bend_v[a]
        for side in range(2):
            zmsg[side, 2 * a:2 * a + 2, :] = tz_v[a, PZ + 2 * side:PZ + 2 * side + 2, :]
        block = accc[2:2 + KX, :, a * SZ:(a + 1) * SZ].reshape(KX * QC, SZ)
        cslots[2, me[2], a * KZ:(a + 1) * KZ, :] = nt(bzc, block)

    def coarse_copy(k, d, slot):
        n = counts[k]
        return pltpu.make_async_remote_copy(
            src_ref=cslots.at[k, slot], dst_ref=cslots.at[k, slot],
            send_sem=cs_sem.at[k, d], recv_sem=cr_sem.at[k, d],
            device_id={axes[k]: lax.rem(me[k] + d, n)}, device_id_type=MESH,
        )

    def exchange(k, source, got):
        for side in range(2):
            @pl.when(has[k][side])
            def _(side=side):
                neighbour_copy(k, side, source(side), got.at[1 - side],
                               ms_sem.at[k, side], mr_sem.at[k, 1 - side]).start()
        for d in range(1, counts[k]):
            coarse_copy(k, d, me[k]).start()
        for side in range(2):
            @pl.when(has[k][side])
            def _(side=side):
                neighbour_copy(k, side, source(side), got.at[1 - side],
                               ms_sem.at[k, side], mr_sem.at[k, 1 - side]).wait_send()

            @pl.when(has[k][1 - side])
            def _(side=side):
                neighbour_copy(k, side, source(side), got.at[1 - side],
                               ms_sem.at[k, side], mr_sem.at[k, 1 - side]).wait_recv()
        for d in range(1, counts[k]):
            coarse_copy(k, d, me[k]).wait_send()
            coarse_copy(k, d, lax.rem(me[k] + counts[k] - d, counts[k])).wait_recv()
        whole = cslots[k, 0]
        for n in range(1, counts[k]):
            whole = whole + cslots[k, n]
        return whole

    whole = exchange(2, lambda side: zmsg.at[side], zgot)
    for a in range(3):
        tz_v[a, 0:2, :] = tz_v[a, 0:2, :] + zgot[0, 2 * a:2 * a + 2, :]
        tz_v[a, PZ - 2:PZ, :] = tz_v[a, PZ - 2:PZ, :] + zgot[1, 2 * a:2 * a + 2, :]
        a_v[a * PZ:(a + 1) * PZ, :] = tz_v[a, 0:PZ, :]

    cslots[1, me[1]] = whole
    whole = exchange(1, lambda side: a_v, agot)
    shape = (EX * QE, EX * PY)
    rows, cols = iota(shape, 0), iota(shape, 1)
    p_same = rows // QE == cols // PY
    q, r = rows % QE, cols % PY
    own = jnp.where(p_same & (q == r + 2), 1.0, 0.0)
    low = jnp.where(p_same & (q == r + PY + 2) & (r < 2), 1.0, 0.0)
    high = jnp.where(p_same & (q == r - (PY - 2)) & (r >= PY - 2), 1.0, 0.0)
    b_v[...] = nn(a_v[...], own) + nn(agot[0], low) + nn(agot[1], high)

    cslots[0, me[0]] = whole
    whole = exchange(0, lambda side: b_v, bgot)
    shape = (PX * PY, EX * PY)
    rows, cols = iota(shape, 0), iota(shape, 1)
    own = jnp.where(cols == rows + 2 * PY, 1.0, 0.0)
    low = jnp.where((cols == rows + (PX + 2) * PY) & (rows < 2 * PY), 1.0, 0.0)
    high = jnp.where((cols == rows - (PX - 2) * PY) & (rows >= (PX - 2) * PY), 1.0, 0.0)
    shape = (KX * QC, KX * QC)
    eye = same(iota(shape, 0), iota(shape, 1))
    for a in range(3):
        part = slice(a * PZ, (a + 1) * PZ)
        out = nt(own, b_v[part]) + nt(low, bgot[0, part]) + nt(high, bgot[1, part])
        fo_ref[a] = out.reshape(PX, PY, PZ)
        out = nt(eye, whole[a * KZ:(a + 1) * KZ]) + bendc[a]
        for p in range(KX):
            co_ref[a, p] = out[p * QC:p * QC + KY, :]


def solution(mesh):
    sizes = tuple(mesh.shape[a] for a in ("gx", "gy", "gz"))

    def step(warped, fixed, fine, coarse):
        SX, SY, SZ = warped.shape
        PX, PY, PZ = SX // SPF, SY // SPF, SZ // SPF
        KX, KY, KZ = coarse.shape[1:]
        QC = -(-KY // 8) * 8
        EX, QE, RZ = PX + 4, 16, PZ + 8
        KC = SPF * SY
        most = max(sizes)
        vmem = pl.BlockSpec(memory_space=pltpu.VMEM)
        hbm = pl.BlockSpec(memory_space=pl.ANY)
        V = pltpu.VMEM
        D = pltpu.SemaphoreType.DMA
        return pl.pallas_call(
            functools.partial(kernel, sizes),
            out_shape=(jax.ShapeDtypeStruct(fine.shape, f32),
                       jax.ShapeDtypeStruct(coarse.shape, f32)),
            in_specs=[hbm, hbm, vmem, vmem],
            out_specs=(vmem, vmem),
            scratch_shapes=[
                V((SX, SY, SZ), f32), V((SX, SY, SZ), f32),
                V((SX + 4, SY + 16, SZ), f32),
                V((2, SX, 2, SZ), f32), V((2, SX, 2, SZ), f32),
                V((2, SY, SZ), f32), V((2, SY, SZ), f32), V((2, SY, SZ), f32),
                V((2, 5 * QE, KC), bf16), V((SPC // SPF, 2, 4 * QC, KC), bf16),
                V((KC, 3 * SZ), bf16), V((KC, 3 * SZ), bf16),
                V((EX, QE, 3 * SZ), f32), V((KX + 4, QC, 3 * SZ), f32),
                V((3, RZ, EX * QE), f32), V((3, RZ, EX * QE), f32),
                V((3, KX * QC, KZ), f32), V((3, KX * QC, KZ), f32),
                V((2, 8, EX * QE), f32), V((2, 8, EX * QE), f32),
                V((3 * PZ, EX * QE), f32), V((2, 3 * PZ, EX * QE), f32),
                V((3 * PZ, EX * PY), f32), V((2, 3 * PZ, EX * PY), f32),
                V((3, most, 3 * KZ, KX * QC), f32),
                D((2, SX // SPF)), D((3, 2)), D((3, 2)), D((3, 2)), D((3, 2)),
                D((3, most)), D((3, most)),
            ],
            compiler_params=pltpu.CompilerParams(
                collective_id=0, has_side_effects=True, vmem_limit_bytes=48 * 2 ** 20
            ),
        )(warped, fixed, fine, coarse)

    in_specs = (P("gx", "gy", "gz"), P("gx", "gy", "gz"), P(None, "gx", "gy", "gz"), P())
    out_specs = (P(None, "gx", "gy", "gz"), P())
    return jax.shard_map(
        step, mesh=mesh, in_specs=in_specs, out_specs=out_specs, check_vma=False
    )
```

time: 160 us -> 40.5 us (0.25)
  blocking collectives: 42.9 us -> 0 us
  starting transfers between devices: 37.7 us -> 0 us
  Pallas kernels: 0 us -> 33.4 us
  waiting for transfers between devices: 24.6 us -> 0 us
  other arithmetic: 23.4 us -> 0 us
  matrix products: 15.2 us -> 0 us
  local copies, waits for them, and re-layouts: 13.9 us -> 6.13 us
    psum x1 -> x0, blocking collectives: 42.9 us -> none  [per_device(): coarse_sum = lax.psum(coarse_part, ('gx', 'gy', 'gz'))]
    ppermute x18 -> x0, starting transfers between devices: 37.7 us -> none  [the longest x9 25.9 us: padded_2(): lax.ppermute(lax.slice_in_dim(block, block.shape[dim] - width, None, axis...]
    pallas_call x0 -> x1, Pallas kernels: none -> 33.4 us  [step(): pl.pallas_call(functools.partial(kernel, sizes), out_shape=(jax.ShapeDtyp...]
    ppermute x18 -> x0, waiting for transfers between devices: 24.6 us -> none  [the longest x9 18.3 us: padded_2(): lax.ppermute(lax.slice_in_dim(block, 0, width, axis=dim), axis, backward)]
    dot_general x6 -> x0, matrix products: 15.2 us -> none  [the longest x2 13 us: project(): section = jnp.einsum('axyz,xp->apyz', force, along_x, precision=highest)]
    another operation x3 -> x0, other arithmetic: 14.7 us -> none  [per_device(): force = jnp.stack(slopes) * difference[None]]
    slice x10 -> x0, local copies, waits for them, and re-layouts: 8.45 us -> none  [the longest x8 5.86 us: padded_2(): lax.slice_in_dim(block, block.shape[dim] - width, None, axis=dim)]
    unnamed x14 -> x10, local copies, waits for them, and re-layouts: 0.67 us -> 6.13 us
  transfers between devices with their start and end apart: 18 -> 0, of which waited for: 8 -> 0; matrix products, arithmetic and copies ran while one was open for 12% -> 0% of each run, Pallas kernels for 0% -> 0%
where the time goes in v1:
time: 40.5 us; the launch traced here: 40.2 us
  Pallas kernels  33.4 us (82%)
  local copies, waits for them, and re-layouts  6.13 us (15%)
  between operations  0.65 us (2%)
    pallas_call x1, Pallas kernels, step(): pl.pallas_call(functools.partial(kernel, sizes), out_shape=(jax.ShapeDtyp...  33.4 us
    unnamed x10, local copies, waits for them, and re-layouts  6.13 us

profile of v1, /device:TPU:0, one launch (start us, length us, event | category | flops | bytes accessed | tf_op | source)
XLA Modules:
  0.0 40.2 jit_solution(17977406853318668382)
XLA Ops:
  0.6 0.0 copy-start
  0.6 1.6 %copy-done = f32[64,64,128]{2,1,0:T(8,128)S(1)} copy-done((f32[64,64,128]{2,1,0:T(8,128)S(1)}, f32[64,64,128]{2,1,0:T(8,128)}, u32[]{:S(2)}) %copy-start) | copy-done | bytes 2097176
  2.2 0.0 copy-start.1
  2.2 1.6 %copy-done.1 = f32[64,64,128]{2,1,0:T(8,128)S(1)} copy-done((f32[64,64,128]{2,1,0:T(8,128)S(1)}, f32[64,64,128]{2,1,0:T(8,128)}, u32[]{:S(2)}) %copy-start.1) | copy-done | bytes 2097176
  3.8 0.0 copy-start.2
  3.8 0.9 %copy-done.2 = f32[3,8,8,16]{3,2,1,0:T(8,128)S(1)} copy-done((f32[3,8,8,16]{3,2,1,0:T(8,128)S(1)}, f32[3,8,8,16]{3,2,1,0:T(8,128)}, u32[]{:S(2)}) %copy-start.2) | copy-done | bytes 12312
  4.7 0.0 copy-start.3
  4.7 0.8 %copy-done.3 = f32[3,8,4,16]{3,2,1,0:T(4,128)S(1)} copy-done((f32[3,8,4,16]{3,2,1,0:T(4,128)S(1)}, f32[3,8,4,16]{3,2,1,0:T(4,128)}, u32[]{:S(2)}) %copy-start.3) | copy-done | bytes 6168
  5.5 33.4 %shard_map.59 = (f32[3,8,8,16]{3,2,1,0:T(8,128)S(1)}, f32[3,8,4,16]{3,2,1,0:T(4,128)S(1)}) custom-call(f32[64,64,128]{2,1,0:T(8,128)S(1)} %copy-done, f32[64,64,128]{2,1,0:T(8,128)S(1)} %copy-done.1, f32[3,8,8,16]{3,2,1,0:T(8,128)S(1)} %copy-done.2, f32[3,8,4,16]{3,2,1,0:T(4,128)S(1)} %copy-done.3), custom_call_target="tpu_custom_call" | custom-call | tf_op jit(solution)/shard_map/pallas_call | solution.py:364
  39.0 0.6 %copy.8 = f32[3,8,8,16]{3,2,1,0:T(8,128)} copy(f32[3,8,8,16]{3,2,1,0:T(8,128)S(1)} %get-tuple-element.4) | data formatting | bytes 24576
  39.6 0.6 %copy.9 = f32[3,8,4,16]{3,2,1,0:T(4,128)} copy(f32[3,8,4,16]{3,2,1,0:T(4,128)S(1)} %get-tuple-element.5) | data formatting | bytes 12288
Async XLA Ops:
  0.6 1.6 %copy-start = (f32[64,64,128]{2,1,0:T(8,128)S(1)}, f32[64,64,128]{2,1,0:T(8,128)}, u32[]{:S(2)}) copy-start(f32[64,64,128]{2,1,0:T(8,128)} %w_hbm.1) | copy-start | bytes 6291460
  2.2 1.6 %copy-start.1 = (f32[64,64,128]{2,1,0:T(8,128)S(1)}, f32[64,64,128]{2,1,0:T(8,128)}, u32[]{:S(2)}) copy-start(f32[64,64,128]{2,1,0:T(8,128)} %f_hbm.1) | copy-start | bytes 6291460
  3.8 0.9 %copy-start.2 = (f32[3,8,8,16]{3,2,1,0:T(8,128)S(1)}, f32[3,8,8,16]{3,2,1,0:T(8,128)}, u32[]{:S(2)}) copy-start(f32[3,8,8,16]{3,2,1,0:T(8,128)} %fc_ref.1) | copy-start | bytes 36868
  4.7 0.8 %copy-start.3 = (f32[3,8,4,16]{3,2,1,0:T(4,128)S(1)}, f32[3,8,4,16]{3,2,1,0:T(4,128)}, u32[]{:S(2)}) copy-start(f32[3,8,4,16]{3,2,1,0:T(4,128)} %cc_ref.1) | copy-start | bytes 18436

commit v2 on v1

v2 whole, which is shorter than its diff:
```python
import functools

import jax
import jax.numpy as jnp
from jax import lax
from jax.experimental import pallas as pl
from jax.experimental.pallas import tpu as pltpu
from jax.sharding import PartitionSpec as P

SPF = 8
SPC = 32
BEND = 0.01
HI = lax.Precision.HIGHEST
MESH = pl.DeviceIdType.MESH
f32 = jnp.float32
bf16 = jnp.bfloat16


def nn(a, b):
    return lax.dot_general(
        a, b, (((1,), (0,)), ((), ())), precision=HI, preferred_element_type=f32
    )


def nt(a, b):
    return lax.dot_general(
        a, b, (((1,), (1,)), ((), ())), precision=HI, preferred_element_type=f32
    )


def spline(t):
    m = jnp.abs(t)
    inner = 2.0 / 3.0 - m * m + 0.5 * m * m * m
    r = 2.0 - m
    outer = r * r * r * (1.0 / 6.0)
    return jnp.where(m < 1.0, inner, jnp.where(m < 2.0, outer, 0.0))


def weight(voxel, point, spacing):
    scaled = (2 * voxel + 1 - spacing * (2 * point + 1)).astype(f32)
    return spline(scaled * (0.5 / spacing))


def iota(shape, axis):
    return lax.broadcasted_iota(jnp.int32, shape, axis)


def diff1(out, inp):
    d = jnp.abs(out - inp)
    return jnp.where(d == 0, -2.0, jnp.where(d == 1, 1.0, 0.0)).astype(f32)


def diff2(out, inp, count):
    d = jnp.abs(out - inp)
    edge = (inp == 0) | (inp == count - 1)
    centre = jnp.where(edge, 5.0, 6.0)
    return jnp.where(
        d == 0, centre, jnp.where(d == 1, -4.0, jnp.where(d == 2, 1.0, 0.0))
    ).astype(f32)


def same(out, inp):
    return jnp.where(out == inp, 1.0, 0.0).astype(f32)


def bend_planes(px, py, qx, qy, cx, cy):
    jx, jy = same(px, qx), same(py, qy)
    tx, ty = diff1(px, qx), diff1(py, qy)
    m0 = diff2(px, qx, cx) * jy + jx * diff2(py, qy, cy) + 2.0 * tx * ty
    m1 = 2.0 * (tx * jy + jx * ty)
    return m0 * BEND, m1 * BEND, jx * jy * BEND


def kernel(sizes, w_hbm, f_hbm, fc_hbm, cc_hbm, fo_ref, co_ref,
           w_v, f_v, fc_ref, cc_ref, s_v, ysend, yrecv, zsend, zrecv, zcorr,
           wf_v, wc_v, fh_v, fl_v,
           accf, accc, tz_v, bend_v, ccp, bendc, zmsg, zgot, a_v, agot, b_v, bgot,
           cslots, load_sem, small_sem, hs_sem, hr_sem, ys_sem, yr_sem,
           ms_sem, mr_sem, cs_sem, cr_sem):
    nx, ny, nz = sizes
    axes = ("gx", "gy", "gz")
    counts = sizes
    me = [lax.axis_index(a) for a in axes]
    SX, SY, SZ = w_v.shape
    PX, PY, PZ = SX // SPF, SY // SPF, SZ // SPF
    KX, KY, KZ = cc_ref.shape[1:]
    EX, QE, QC = PX + 4, 2 * PY, accc.shape[1]
    cells = SX // SPF
    lanes = 3 * SZ

    loads = []
    for c in range(cells):
        part = pl.ds(c * SPF, SPF)
        loads.append((
            pltpu.make_async_copy(w_hbm.at[part], w_v.at[part], load_sem.at[0, c]),
            pltpu.make_async_copy(f_hbm.at[part], f_v.at[part], load_sem.at[1, c]),
        ))
    small = (pltpu.make_async_copy(fc_hbm, fc_ref, small_sem.at[0]),
             pltpu.make_async_copy(cc_hbm, cc_ref, small_sem.at[1]))
    order = [0, cells - 1] + list(range(1, cells - 1))
    for c in order:
        loads[c][0].start()
        loads[c][1].start()
    for copy in small:
        copy.start()

    zero_plane = jnp.zeros((2, SY, SZ), f32)
    s_v[0:2, 8:8 + SY, :] = zero_plane
    s_v[SX + 2:SX + 4, 8:8 + SY, :] = zero_plane
    yrecv[...] = jnp.zeros(yrecv.shape, f32)
    zrecv[...] = jnp.zeros(zrecv.shape, f32)
    zgot[...] = jnp.zeros(zgot.shape, f32)
    agot[...] = jnp.zeros(agot.shape, f32)
    bgot[...] = jnp.zeros(bgot.shape, f32)

    barrier = pltpu.get_barrier_semaphore()
    total = 0
    for k, a in enumerate(axes):
        for d in range(1, counts[k]):
            pl.semaphore_signal(
                barrier, inc=1, device_id={a: lax.rem(me[k] + d, counts[k])}, device_id_type=MESH
            )
            total += 1

    def split_store(ref, index, value):
        high = value.astype(bf16)
        ref[index + (0,)] = high
        ref[index + (1,)] = (value - high.astype(f32)).astype(bf16)

    KC = SPF * SY
    def ext_q(q):
        return jnp.where(q < PY, q, jnp.where(q < PY + 2, q - PY - 2, q - 2))

    rows, cols = iota((5 * QE, KC), 0), iota((5 * QE, KC), 1)
    split_store(wf_v, (), weight(cols // SY, rows // QE - 2, SPF)
                * weight(cols % SY, ext_q(rows % QE), SPF))
    rows, cols = iota((4 * QC, KC), 0), iota((4 * QC, KC), 1)
    along_y = weight(cols % SY + me[1] * SY, rows % QC, SPC)
    for ph in range(SPC // SPF):
        first = -2 if ph < SPC // SPF // 2 else -1
        split_store(wc_v, (ph,),
                    weight(cols // SY + ph * SPF, rows // QC + first, SPC) * along_y)

    pl.semaphore_wait(barrier, total)

    has = [(me[k] > 0, me[k] < counts[k] - 1) for k in range(3)]
    pieces = ys_sem.shape[1]
    each = SX // pieces

    def halo(k, side, piece=0):
        if k == 1:
            part = pl.ds(piece * each, each)
            return neighbour_copy(
                k, side, ysend.at[side, part], yrecv.at[1 - side, part],
                ys_sem.at[side, piece], yr_sem.at[1 - side, piece])
        if k == 0:
            src = s_v.at[pl.ds(2 if side == 0 else SX, 2), pl.ds(8, SY), :]
            dst = s_v.at[pl.ds(SX + 2 if side == 0 else 0, 2), pl.ds(8, SY), :]
        else:
            src, dst = zsend.at[side], zrecv.at[1 - side]
        return neighbour_copy(k, side, src, dst, hs_sem.at[k, side], hr_sem.at[k, 1 - side])

    def neighbour_copy(k, side, src, dst, send, recv):
        other = me[k] - 1 if side == 0 else me[k] + 1
        return pltpu.make_async_remote_copy(
            src_ref=src, dst_ref=dst, send_sem=send, recv_sem=recv,
            device_id={axes[k]: other}, device_id_type=MESH,
        )

    def start_halo(k, side, piece=0):
        @pl.when(has[k][side])
        def _():
            halo(k, side, piece).start()

    lane = iota((SY, SZ), 1)

    def one_slab(x, carry):
        low, high = carry
        s = w_v[x] + f_v[x]
        s_v[x + 2, 8:8 + SY, :] = s
        ysend[0, x] = s[0:2]
        ysend[1, x] = s[SY - 2:SY]
        here = lane // 2 == x
        low = jnp.where(here, pltpu.roll(s, 2 * x, 1), low)
        high = jnp.where(here, pltpu.roll(s, lax.rem(2 * x + 2, SZ), 1), high)
        return low, high

    carry = (jnp.zeros((SY, SZ), f32), jnp.zeros((SY, SZ), f32))
    done = set()
    sent = set()
    for c in order:
        for copy in loads[c]:
            copy.wait()
        carry = lax.fori_loop(c * SPF, (c + 1) * SPF, one_slab, carry)
        done.add(c)
        for piece in range(pieces):
            inside = range(piece * each // SPF, (piece + 1) * each // SPF)
            if piece not in sent and all(n in done for n in inside):
                sent.add(piece)
                start_halo(1, 0, piece)
                start_halo(1, 1, piece)
        if c == 0:
            start_halo(0, 0)
        if c == cells - 1:
            start_halo(0, 1)
    zsend[0] = carry[0]
    zsend[1] = carry[1]
    start_halo(2, 0)
    start_halo(2, 1)

    accf[...] = jnp.zeros(accf.shape, f32)
    accc[...] = jnp.zeros(accc.shape, f32)
    for copy in small:
        copy.wait()
    shape = (EX * QE, PX * PY)
    rows, cols = iota(shape, 0), iota(shape, 1)
    ox, oy = me[0] * PX, me[1] * PY
    outer, inner = rows // (EX * PY), rows % (EX * PY)
    planes = bend_planes(inner // PY - 2 + ox, ext_q(inner % PY + PY * outer) + oy,
                         cols // PY + ox, cols % PY + oy, PX * nx, PY * ny)
    RZ = tz_v.shape[2]

    def ext_point(row):
        return jnp.where(row < PZ, row, jnp.where(row < PZ + 2, row - PZ - 2, row - 2))

    oz = me[2] * PZ
    zr, zc = ext_point(iota((RZ, PZ), 0)) + oz, iota((RZ, PZ), 1) + oz
    along = (same(zr, zc), diff1(zr, zc), diff2(zr, zc, PZ * nz))
    for a in range(3):
        block = fc_ref[a].reshape(PX * PY, PZ)
        factors = [nn(plane, block) for plane in planes]
        for half in range(2):
            part = slice(half * EX * PY, (half + 1) * EX * PY)
            bend_v[half, a] = (nt(along[0], factors[0][part]) + nt(along[1], factors[1][part])
                               + nt(along[2], factors[2][part]))
    shape = (KX * QC, KX * QC)
    rows, cols = iota(shape, 0), iota(shape, 1)
    planes = bend_planes(rows // QC, rows % QC, cols // QC, cols % QC, KX, KY)
    zr, zc = iota((KZ, KZ), 0), iota((KZ, KZ), 1)
    for a in range(3):
        for p in range(KX):
            ccp[a, p * QC:p * QC + KY, :] = cc_ref[a, p]
        block = ccp[a]
        bendc[a] = (nn(planes[0], block) + nn(planes[1], nn(block, diff1(zr, zc)))
                    + BEND * nn(block, diff2(zr, zc, KZ)))

    for k in (0, 1, 2):
        for side in range(2):
            for piece in range(pieces if k == 1 else 1):
                @pl.when(has[k][side])
                def _(k=k, side=side, piece=piece):
                    halo(k, side, piece).wait_send()

                @pl.when(has[k][1 - side])
                def _(k=k, side=side, piece=piece):
                    halo(k, side, piece).wait_recv()

    even = lane % 2 == 0
    dl = zrecv[0] - zsend[1]
    dh = zrecv[1] - zsend[0]
    zcorr[0] = jnp.where(even, dl - 8.0 * pltpu.roll(dl, SZ - 1, 1), dl)
    zcorr[1] = jnp.where(even, -dh, 8.0 * pltpu.roll(dh, 1, 1) - dh)

    def forces(i):
        slot = i % 2
        for xx in range(SPF):
            x = i * SPF + xx
            s_v[x + 2, 6:8, :] = yrecv[0, x]
            s_v[x + 2, 8 + SY:10 + SY, :] = yrecv[1, x]
            d = w_v[x] - f_v[x]
            s = s_v[x + 2, 8:8 + SY, :]
            gx = (s_v[x, 8:8 + SY, :] - s_v[x + 4, 8:8 + SY, :]
                  + 8.0 * (s_v[x + 3, 8:8 + SY, :] - s_v[x + 1, 8:8 + SY, :]))
            gy = (s_v[x + 2, 6:6 + SY, :] - s_v[x + 2, 10:10 + SY, :]
                  + 8.0 * (s_v[x + 2, 9:9 + SY, :] - s_v[x + 2, 7:7 + SY, :]))
            gz = (pltpu.roll(s, 2, 1) - pltpu.roll(s, SZ - 2, 1)
                  + 8.0 * (pltpu.roll(s, SZ - 1, 1) - pltpu.roll(s, 1, 1)))
            corr = jnp.where(lane < 2, pltpu.roll(zcorr[0], (SZ - 2 * x) % SZ, 1), 0.0)
            corr = jnp.where(lane >= SZ - 2,
                             pltpu.roll(zcorr[1], (2 * SZ - 2 - 2 * x) % SZ, 1), corr)
            gz = gz + corr
            for a, g in enumerate((gx, gy, gz)):
                force = g * d
                high = force.astype(bf16)
                fh_v[slot, xx * SY:(xx + 1) * SY, a * SZ:(a + 1) * SZ] = high
                fl_v[slot, xx * SY:(xx + 1) * SY, a * SZ:(a + 1) * SZ] = (
                    force - high.astype(f32)).astype(bf16)

    def gather(i):
        slot = i % 2
        k, ph = divmod(i, SPC // SPF)
        many = 5 * QE + 4 * QC
        weights = jnp.concatenate([wf_v[0], wc_v[ph, 0], wf_v[1], wc_v[ph, 1]], axis=0)
        both = jnp.dot(weights, fh_v[slot], preferred_element_type=f32)
        out = both[:many] + both[many:] + jnp.dot(
            weights[:many], fl_v[slot], preferred_element_type=f32)
        fine = out[:5 * QE].reshape(5, 2, PY, lanes)
        accf[0, i:i + 5] += fine[:, 0]
        accf[1, i:i + 5] += fine[:, 1]
        at = me[0] * (SX // SPC) + k + (1 if ph >= SPC // SPF // 2 else 0)
        accc[pl.ds(at, 4)] += out[5 * QE:].reshape(4, QC, lanes)

    forces(0)
    for i in range(cells):
        if i + 1 < cells:
            forces(i + 1)
        gather(i)

    rows, cols = iota((RZ, SZ), 0), iota((RZ, SZ), 1)
    bz = weight(cols, ext_point(rows), SPF) * (SPF ** -1.5 / 24.0)
    rows, cols = iota((KZ, SZ), 0), iota((KZ, SZ), 1)
    bzc = weight(cols + me[2] * SZ, rows, SPC) * (SPC ** -1.5 / 24.0)
    for a in range(3):
        for half in range(2):
            block = accf[half, :, :, a * SZ:(a + 1) * SZ].reshape(EX * PY, SZ)
            tz_v[half, a] = nt(bz, block) + bend_v[half, a]
            for side in range(2):
                zmsg[side, half, 2 * a:2 * a + 2, :] = tz_v[
                    half, a, PZ + 2 * side:PZ + 2 * side + 2, :]
    blocks = [accc[2:2 + KX, :, a * SZ:(a + 1) * SZ].reshape(KX * QC, SZ) for a in range(3)]
    cslots[2, me[2]] = nt(bzc, jnp.concatenate(blocks, axis=0))

    def coarse_copy(k, d, slot):
        n = counts[k]
        return pltpu.make_async_remote_copy(
            src_ref=cslots.at[k, slot], dst_ref=cslots.at[k, slot],
            send_sem=cs_sem.at[k, d], recv_sem=cr_sem.at[k, d],
            device_id={axes[k]: lax.rem(me[k] + d, n)}, device_id_type=MESH,
        )

    def exchange(k, source, got):
        for side in range(2):
            @pl.when(has[k][side])
            def _(side=side):
                neighbour_copy(k, side, source(side), got.at[1 - side],
                               ms_sem.at[k, side], mr_sem.at[k, 1 - side]).start()
        for d in range(1, counts[k]):
            coarse_copy(k, d, me[k]).start()
        for side in range(2):
            @pl.when(has[k][side])
            def _(side=side):
                neighbour_copy(k, side, source(side), got.at[1 - side],
                               ms_sem.at[k, side], mr_sem.at[k, 1 - side]).wait_send()

            @pl.when(has[k][1 - side])
            def _(side=side):
                neighbour_copy(k, side, source(side), got.at[1 - side],
                               ms_sem.at[k, side], mr_sem.at[k, 1 - side]).wait_recv()
        for d in range(1, counts[k]):
            coarse_copy(k, d, me[k]).wait_send()
            coarse_copy(k, d, lax.rem(me[k] + counts[k] - d, counts[k])).wait_recv()
        whole = cslots[k, 0]
        for n in range(1, counts[k]):
            whole = whole + cslots[k, n]
        return whole

    whole = exchange(2, lambda side: zmsg.at[side], zgot)
    for half in range(2):
        for a in range(3):
            tz_v[half, a, 0:2, :] = tz_v[half, a, 0:2, :] + zgot[0, half, 2 * a:2 * a + 2, :]
            tz_v[half, a, PZ - 2:PZ, :] = (
                tz_v[half, a, PZ - 2:PZ, :] + zgot[1, half, 2 * a:2 * a + 2, :])
            a_v[half, a * PZ:(a + 1) * PZ, :] = tz_v[half, a, 0:PZ, :]

    cslots[1, me[1]] = whole
    whole = exchange(1, lambda side: a_v.at[1], agot)
    shape = (EX * PY, EX * PY)
    rows, cols = iota(shape, 0), iota(shape, 1)
    p_same = rows // PY == cols // PY
    q, r = rows % PY, cols % PY
    low = jnp.where(p_same & (q == r + 2) & (r < 2), 1.0, 0.0)
    high = jnp.where(p_same & (q == r - (PY - 2)) & (r >= PY - 2), 1.0, 0.0)
    b_v[...] = a_v[0] + nn(agot[0], low) + nn(agot[1], high)

    cslots[0, me[0]] = whole
    whole = exchange(0, lambda side: b_v, bgot)
    shape = (PX * PY, EX * PY)
    rows, cols = iota(shape, 0), iota(shape, 1)
    own = jnp.where(cols == rows + 2 * PY, 1.0, 0.0)
    low = jnp.where((cols == rows + (PX + 2) * PY) & (rows < 2 * PY), 1.0, 0.0)
    high = jnp.where((cols == rows - (PX - 2) * PY) & (rows >= (PX - 2) * PY), 1.0, 0.0)
    shape = (3 * KX * QC, 3 * KX * QC)
    turned = nt(same(iota(shape, 0), iota(shape, 1)), whole)
    for a in range(3):
        part = slice(a * PZ, (a + 1) * PZ)
        out = nt(own, b_v[part]) + nt(low, bgot[0, part]) + nt(high, bgot[1, part])
        fo_ref[a] = out.reshape(PX, PY, PZ)
        out = turned[a * KX * QC:(a + 1) * KX * QC] + bendc[a]
        for p in range(KX):
            co_ref[a, p] = out[p * QC:p * QC + KY, :]


def solution(mesh):
    sizes = tuple(mesh.shape[a] for a in ("gx", "gy", "gz"))

    def step(warped, fixed, fine, coarse):
        SX, SY, SZ = warped.shape
        PX, PY, PZ = SX // SPF, SY // SPF, SZ // SPF
        KX, KY, KZ = coarse.shape[1:]
        QC = KY
        EX, QE, RZ = PX + 4, 2 * PY, PZ + 8
        KC = SPF * SY
        most = max(sizes)
        vmem = pl.BlockSpec(memory_space=pltpu.VMEM)
        hbm = pl.BlockSpec(memory_space=pltpu.HBM)
        V = pltpu.VMEM
        D = pltpu.SemaphoreType.DMA
        return pl.pallas_call(
            functools.partial(kernel, sizes),
            out_shape=(jax.ShapeDtypeStruct(fine.shape, f32),
                       jax.ShapeDtypeStruct(coarse.shape, f32)),
            in_specs=[hbm] * 4,
            out_specs=(vmem, vmem),
            scratch_shapes=[
                V((SX, SY, SZ), f32), V((SX, SY, SZ), f32),
                V((3, PX, PY, PZ), f32), V(coarse.shape, f32),
                V((SX + 4, SY + 16, SZ), f32),
                V((2, SX, 2, SZ), f32), V((2, SX, 2, SZ), f32),
                V((2, SY, SZ), f32), V((2, SY, SZ), f32), V((2, SY, SZ), f32),
                V((2, 5 * QE, KC), bf16), V((SPC // SPF, 2, 4 * QC, KC), bf16),
                V((2, KC, 3 * SZ), bf16), V((2, KC, 3 * SZ), bf16),
                V((2, EX, PY, 3 * SZ), f32), V((KX + 4, QC, 3 * SZ), f32),
                V((2, 3, RZ, EX * PY), f32), V((2, 3, RZ, EX * PY), f32),
                V((3, KX * QC, KZ), f32), V((3, KX * QC, KZ), f32),
                V((2, 2, 8, EX * PY), f32), V((2, 2, 8, EX * PY), f32),
                V((2, 3 * PZ, EX * PY), f32), V((2, 3 * PZ, EX * PY), f32),
                V((3 * PZ, EX * PY), f32), V((2, 3 * PZ, EX * PY), f32),
                V((3, most, KZ, 3 * KX * QC), f32),
                D((2, SX // SPF)), D((2,)), D((3, 2)), D((3, 2)), D((2, 4)), D((2, 4)),
                D((3, 2)), D((3, 2)), D((3, most)), D((3, most)),
            ],
            compiler_params=pltpu.CompilerParams(
                collective_id=0, has_side_effects=True, vmem_limit_bytes=48 * 2 ** 20
            ),
        )(warped, fixed, fine, coarse)

    in_specs = (P("gx", "gy", "gz"), P("gx", "gy", "gz"), P(None, "gx", "gy", "gz"), P())
    out_specs = (P(None, "gx", "gy", "gz"), P())
    return jax.shard_map(
        step, mesh=mesh, in_specs=in_specs, out_specs=out_specs, check_vma=False
    )
```

time: 40.5 us -> 38.2 us (0.943)
  Pallas kernels: 33.4 us -> 31.2 us
    pallas_call x1, Pallas kernels: 33.4 us -> 31.2 us  [step(): pl.pallas_call(functools.partial(kernel, sizes), out_shape=(jax.ShapeDtyp...]
where the time goes in v2:
time: 38.2 us; the launch traced here: 38 us
  Pallas kernels  31.2 us (82%)
  local copies, waits for them, and re-layouts  6.13 us (16%)
  between operations  0.65 us (2%)
    pallas_call x1, Pallas kernels, step(): pl.pallas_call(functools.partial(kernel, sizes), out_shape=(jax.ShapeDtyp...  31.2 us
    unnamed x10, local copies, waits for them, and re-layouts  6.13 us

profile of v2, /device:TPU:0, one launch (start us, length us, event | category | flops | bytes accessed | tf_op | source)
XLA Modules:
  0.0 38.0 jit_solution(5699705058459192564)
XLA Ops:
  0.6 0.0 copy-start
  0.6 1.6 %copy-done = f32[64,64,128]{2,1,0:T(8,128)S(1)} copy-done((f32[64,64,128]{2,1,0:T(8,128)S(1)}, f32[64,64,128]{2,1,0:T(8,128)}, u32[]{:S(2)}) %copy-start) | copy-done | bytes 2097176
  2.2 0.0 copy-start.1
  2.2 1.6 %copy-done.1 = f32[64,64,128]{2,1,0:T(8,128)S(1)} copy-done((f32[64,64,128]{2,1,0:T(8,128)S(1)}, f32[64,64,128]{2,1,0:T(8,128)}, u32[]{:S(2)}) %copy-start.1) | copy-done | bytes 2097176
  3.8 0.0 copy-start.2
  3.8 0.9 %copy-done.2 = f32[3,8,8,16]{3,2,1,0:T(8,128)S(1)} copy-done((f32[3,8,8,16]{3,2,1,0:T(8,128)S(1)}, f32[3,8,8,16]{3,2,1,0:T(8,128)}, u32[]{:S(2)}) %copy-start.2) | copy-done | bytes 12312
  4.7 0.0 copy-start.3
  4.7 0.8 %copy-done.3 = f32[3,8,4,16]{3,2,1,0:T(4,128)S(1)} copy-done((f32[3,8,4,16]{3,2,1,0:T(4,128)S(1)}, f32[3,8,4,16]{3,2,1,0:T(4,128)}, u32[]{:S(2)}) %copy-start.3) | copy-done | bytes 6168
  5.5 31.2 %shard_map.59 = (f32[3,8,8,16]{3,2,1,0:T(8,128)S(1)}, f32[3,8,4,16]{3,2,1,0:T(4,128)S(1)}) custom-call(f32[64,64,128]{2,1,0:T(8,128)S(1)} %copy-done, f32[64,64,128]{2,1,0:T(8,128)S(1)} %copy-done.1, f32[3,8,8,16]{3,2,1,0:T(8,128)S(1)} %copy-done.2, f32[3,8,4,16]{3,2,1,0:T(4,128)S(1)} %copy-done.3), custom_call_target="tpu_custom_call" | custom-call | tf_op jit(solution)/shard_map/pallas_call | solution.py:408
  36.7 0.6 %copy.8 = f32[3,8,8,16]{3,2,1,0:T(8,128)} copy(f32[3,8,8,16]{3,2,1,0:T(8,128)S(1)} %get-tuple-element.4) | data formatting | bytes 24576
  37.4 0.6 %copy.9 = f32[3,8,4,16]{3,2,1,0:T(4,128)} copy(f32[3,8,4,16]{3,2,1,0:T(4,128)S(1)} %get-tuple-element.5) | data formatting | bytes 12288
Async XLA Ops:
  0.6 1.6 %copy-start = (f32[64,64,128]{2,1,0:T(8,128)S(1)}, f32[64,64,128]{2,1,0:T(8,128)}, u32[]{:S(2)}) copy-start(f32[64,64,128]{2,1,0:T(8,128)} %w_hbm.1) | copy-start | bytes 6291460
  2.2 1.6 %copy-start.1 = (f32[64,64,128]{2,1,0:T(8,128)S(1)}, f32[64,64,128]{2,1,0:T(8,128)}, u32[]{:S(2)}) copy-start(f32[64,64,128]{2,1,0:T(8,128)} %f_hbm.1) | copy-start | bytes 6291460
  3.8 0.9 %copy-start.2 = (f32[3,8,8,16]{3,2,1,0:T(8,128)S(1)}, f32[3,8,8,16]{3,2,1,0:T(8,128)}, u32[]{:S(2)}) copy-start(f32[3,8,8,16]{3,2,1,0:T(8,128)} %fc_hbm.1) | copy-start | bytes 36868
  4.7 0.8 %copy-start.3 = (f32[3,8,4,16]{3,2,1,0:T(4,128)S(1)}, f32[3,8,4,16]{3,2,1,0:T(4,128)}, u32[]{:S(2)}) copy-start(f32[3,8,4,16]{3,2,1,0:T(4,128)} %cc_hbm.1) | copy-start | bytes 18436

commit v3 on v2

--- a/solution.py
+++ b/solution.py
@@ -430,7 +430,7 @@
                 D((3, 2)), D((3, 2)), D((3, most)), D((3, most)),
             ],
             compiler_params=pltpu.CompilerParams(
-                collective_id=0, has_side_effects=True, vmem_limit_bytes=48 * 2 ** 20
+                collective_id=0, has_side_effects=True, vmem_limit_bytes=66000000
             ),
         )(warped, fixed, fine, coarse)
 

time: 38.2 us -> 35.3 us (0.924)
  local copies, waits for them, and re-layouts: 6.13 us -> 2.96 us
    unnamed x10 -> x2, local copies, waits for them, and re-layouts: 6.13 us -> 2.96 us
where the time goes in v3:
time: 35.3 us; the launch traced here: 35.1 us
  Pallas kernels  31.5 us (89%)
  local copies, waits for them, and re-layouts  2.96 us (8%)
  between operations  0.64 us (2%)
    pallas_call x1, Pallas kernels, step(): pl.pallas_call(functools.partial(kernel, sizes), out_shape=(jax.ShapeDtyp...  31.5 us
    unnamed x2, local copies, waits for them, and re-layouts  2.96 us

profile of v3, /device:TPU:0, one launch (start us, length us, event | category | flops | bytes accessed | tf_op | source)
XLA Modules:
  0.0 35.1 jit_solution(13479825486412277418)
XLA Ops:
  0.6 31.5 %shard_map.59 = (f32[3,8,8,16]{3,2,1,0:T(8,128)}, f32[3,8,4,16]{3,2,1,0:T(4,128)}) custom-call(f32[64,64,128]{2,1,0:T(8,128)} %w_hbm.1, f32[64,64,128]{2,1,0:T(8,128)} %f_hbm.1, f32[3,8,8,16]{3,2,1,0:T(8,128)} %fc_hbm.1, f32[3,8,4,16]{3,2,1,0:T(4,128)} %cc_hbm.1), custom_call_target="tpu_custom_call" | custom-call | tf_op jit(solution)/shard_map/pallas_call | solution.py:408
  32.1 1.5 %copy.8 = f32[3,8,8,16]{3,2,1,0:T(8,128)} copy(f32[3,8,8,16]{3,2,1,0:T(8,128)} %get-tuple-element.4) | data formatting | bytes 24576
  33.7 1.4 %copy.9 = f32[3,8,4,16]{3,2,1,0:T(4,128)} copy(f32[3,8,4,16]{3,2,1,0:T(4,128)} %get-tuple-element.5) | data formatting | bytes 12288
